TPU v7x, 32 devices: a whole 2x2x4 slice. The times are simulated.
32 devices in a mesh: cuts: 4 (over z), dev: 8 (over y, x, core).
Axes of the slice: x: 2, y: 2, z: 4, core: 2. Of those that a mesh axis runs over, the one named last changes fastest.
Arguments:
- inputs: bfloat16 [16384, 3072], P(('cuts', 'dev')), may hold values from -6 to 6
- cotangent: bfloat16 [16384, 512], P(('cuts', 'dev')), may hold values from -0.29882812 to 0.29882812
- errors: bfloat16 [32, 3072, 512], P(('cuts', 'dev')), may hold values from -6 to 6
- previous_q: float32 [512, 64], replicated, may hold values from -0.25 to 0.25
Outputs:
- new_errors: bfloat16 [32, 3072, 512], P(('cuts', 'dev'))
- p_hat: float32 [3072, 64], replicated
- q_mean: float32 [512, 64], replicated
All inputs are finite; a program needn't handle non-finite values.
Results may differ from a plain program's by a relative error of at most 0.001.
Values sent between devices are 32-bit elements; how exact they have to be, the bound alone decides.
No kernel may reach another device: no remote copies, remote signals or barrier semaphores. Data moves between devices by JAX's collectives and lax.ppermute only.
A program may use at most 64 MiB of HBM per device.

v0:
```python
import jax
import jax.numpy as jnp
from jax import lax
from jax.sharding import PartitionSpec as P

HI = lax.Precision.HIGHEST


def solve_factor(gram, p_rows):
    lower = jnp.linalg.cholesky(gram)
    return lax.linalg.triangular_solve(lower, p_rows, left_side=False, lower=True, transpose_a=True)


def contract_rows(left, right):
    return lax.dot_general(
        left, right, (((0,), (0,)), ((), ())), precision=HI, preferred_element_type=jnp.float32
    )


def body(inputs, cotangent, errors, previous_q):
    grad = lax.dot_general(
        inputs, cotangent, (((0,), (0,)), ((), ())), preferred_element_type=jnp.float32
    )
    merged = grad + errors[0].astype(jnp.float32)
    devices = lax.axis_size("cuts") * lax.axis_size("dev")
    p_share = lax.psum_scatter(
        jnp.dot(merged, previous_q, precision=HI), "dev", scatter_dimension=0, tiled=True
    )
    p_share = lax.psum(p_share, "cuts")
    gram = lax.psum(contract_rows(p_share, p_share), "dev")
    hat_share = solve_factor(gram, p_share)
    p_hat = lax.all_gather(hat_share, "dev", axis=0, tiled=True)
    q_share = lax.psum_scatter(contract_rows(merged, p_hat), "dev", scatter_dimension=0, tiled=True)
    q_share = lax.psum(q_share, "cuts")
    q_sum = lax.all_gather(q_share, "dev", axis=0, tiled=True)
    q_mean = q_sum / devices
    approx = jnp.dot(p_hat, q_mean.T, precision=HI)
    new_errors = (merged - approx).astype(jnp.bfloat16)[None]
    return (new_errors, p_hat, q_mean)


def solution(mesh):
    in_specs = (
        P(("cuts", "dev"), None),
        P(("cuts", "dev"), None),
        P(("cuts", "dev"), None, None),
        P(),
    )
    out_specs = (P(("cuts", "dev"), None, None), P(), P())
    return jax.shard_map(body, mesh=mesh, in_specs=in_specs, out_specs=out_specs, check_vma=False)
```

profile of v0, /device:TPU:0, one launch (start us, length us, event | category | flops | bytes accessed | tf_op | source)
XLA Modules:
  0.0 238.6 jit_solution(2747192408776111508)
XLA Ops:
  7.2 0.0 copy-start
  7.2 0.0 copy-start.3
  7.2 0.0 reduce-scatter.3.cloned.1.call-start
  7.2 1.8 copy-done
  9.1 4.0 %convert_add_fusion = f32[3072,512]{1,0:T(8,128)S(1)} fusion(bf16[512,3072]{1,0:T(8,128)(2,1)S(1)} %copy-done, bf16[512,512]{1,0:T(8,128)(2,1)} %param.5, bf16[1,3072,512]{2,1,0:T(8,128)(2,1)} %param.6), kind=kOutput, calls=%fused_computation | convolution fusion | flops 1613758464 | bytes 13107200 | tf_op jit(solution)/shard_map/dot_general | solution.py:21
  13.0 0.0 copy-start.1
  13.1 2.7 %copy-done.1 = f32[3072,512]{1,0:T(8,128)} copy-done((f32[3072,512]{1,0:T(8,128)}, f32[3072,512]{1,0:T(8,128)S(1)}, u32[]{:S(2)}) %copy-start.1) | copy-done | bytes 6291480
  15.7 0.0 copy-done.3
  15.7 7.1 %fusion.5 = f32[3072,64]{0,1:T(8,128)} fusion(f32[3072,512]{1,0:T(8,128)S(1)} %convert_add_fusion, f32[512,64]{0,1:T(8,128)S(1)} %copy-done.3), kind=kOutput, calls=%fused_computation.14 | convolution fusion | flops 1207959552 | bytes 7208960 | tf_op jit(solution)/shard_map/dot_general | solution.py:27
  22.8 0.0 reduce-scatter.3.cloned.1.call-update
  22.8 0.0 all-reduce.2.cloned.1.call-start
  22.9 37.8 %reduce-scatter.3.cloned.1.call-done = f32[384,64]{0,1:T(8,128)} async-done(((f32[3072,64]{0,1:T(8,128)}), f32[384,64]{0,1:T(8,128)}) %reduce-scatter.3.cloned.1.call-update) | async-done | bytes 98320 | tf_op jit(solution)/shard_map/reduce_scatter | solution.py:26
  60.6 0.0 all-reduce.2.cloned.1.call-update
  60.7 0.0 reduce-scatter.5.cloned.1.call-start
  60.7 36.7 %all-reduce.2.cloned.1.call-done = f32[384,64]{0,1:T(8,128)} async-done(((f32[384,64]{0,1:T(8,128)}), f32[384,64]{0,1:T(8,128)}) %all-reduce.2.cloned.1.call-update) | async-done | bytes 98320 | tf_op jit(solution)/shard_map/psum | solution.py:29
  97.4 1.2 fusion.6
  98.7 22.4 %psum.22 = f32[64,64]{0,1:T(8,128)S(1)} all-reduce(f32[64,64]{0,1:T(8,128)S(1)} %fusion.6), channel_id=1, replica_groups=mesh['cuts'=4,'dev'=8] {'dev'}, use_global_device_ids=true, to_apply=%region_2.0 | all-reduce | flops 4096 | bytes 32768 | tf_op jit(solution)/shard_map/psum | solution.py:30
  121.0 0.1 copy.8
  121.1 5.8 %cholesky.16 = f32[64,64]{1,0:T(8,128)S(1)} custom-call(f32[64,64]{1,0:T(8,128)S(1)} %fusion.4), custom_call_target="Cholesky" | custom-call | tf_op jit(solution)/shard_map/jit(cholesky)/cholesky | solution.py:10
  127.0 0.6 compare_reduce_fusion
  127.6 0.7 fusion.1
  128.3 4.9 %custom-call.6 = f32[1,64,64]{1,2,0:T(8,128)S(1)} custom-call(f32[1,64,64]{2,1,0:T(8,128)S(1)} %fusion.1), custom_call_target="InvertDiagBlocksLowerTriangular" | custom-call | tf_op jit(solution)/shard_map/triangular_solve | solution.py:11
  133.2 1.2 fusion.2
  134.4 11.1 %all_gather.6 = f32[3072,64]{0,1:T(8,128)S(1)} all-gather(f32[384,64]{0,1:T(8,128)S(1)} %fusion.2), channel_id=1, replica_groups=mesh['cuts'=4,'dev'=8] {'dev'}, dimensions={0}, use_global_device_ids=true | all-gather | bytes 884736 | tf_op jit(solution)/shard_map/all_gather | solution.py:32
  145.5 0.0 copy-start.2
  145.5 0.9 copy-done.2
  146.4 12.7 %fusion.7 = f32[512,64]{1,0:T(8,128)} fusion(f32[3072,512]{1,0:T(8,128)} %copy-done.1, f32[3072,64]{0,1:T(8,128)S(1)} %all_gather.6), kind=kOutput, calls=%fused_computation.16 | convolution fusion | flops 1207959552 | bytes 7208960 | tf_op jit(solution)/shard_map/dot_general | solution.py:15
  159.1 0.0 reduce-scatter.5.cloned.1.call-update
  159.1 32.7 %reduce-scatter.5.cloned.1.call-done = f32[64,64]{1,0:T(8,128)} async-done(((f32[512,64]{1,0:T(8,128)}), f32[64,64]{1,0:T(8,128)}) %reduce-scatter.5.cloned.1.call-update) | async-done | bytes 16400 | tf_op jit(solution)/shard_map/reduce_scatter | solution.py:33
  191.8 19.6 %psum.23 = f32[64,64]{1,0:T(8,128)S(1)} all-reduce(f32[64,64]{1,0:T(8,128)} %reduce-scatter.5.cloned.1.call-done), channel_id=1, replica_groups=mesh['cuts'=4,'dev'=8] {'cuts'}, use_global_device_ids=true, to_apply=%region_6.7 | all-reduce | flops 4096 | bytes 32768 | tf_op jit(solution)/shard_map/psum | solution.py:34
  211.4 9.2 %all_gather.7 = f32[512,64]{1,0:T(8,128)S(1)} all-gather(f32[64,64]{1,0:T(8,128)S(1)} %psum.23), channel_id=1, replica_groups=mesh['cuts'=4,'dev'=8] {'dev'}, dimensions={0}, use_global_device_ids=true | all-gather | bytes 147456 | tf_op jit(solution)/shard_map/all_gather | solution.py:35
  220.6 8.6 %fusion = bf16[1,3072,512]{2,1,0:T(8,128)(2,1)} fusion(f32[3072,512]{1,0:T(8,128)} %copy-done.1, f32[3072,64]{0,1:T(8,128)} %copy-done.2, f32[512,64]{1,0:T(8,128)S(1)} %all_gather.7), kind=kOutput, calls=%fused_computation.2 | convolution fusion | flops 1211138048 | bytes 10354688 | tf_op jit(solution)/shard_map/dot_general | solution.py:37
  229.2 0.8 copy.9
  230.0 2.1 copy.13
  (3 shorter events, 0.1 us)
Async XLA Ops:
  7.2 1.9 copy-start
  7.2 8.5 %copy-start.3 = (f32[512,64]{0,1:T(8,128)S(1)}, f32[512,64]{0,1:T(8,128)}, u32[]{:S(2)}) copy-start(f32[512,64]{0,1:T(8,128)} %param.7) | copy-start | bytes 393220
  7.2 53.5 %reduce-scatter.3.cloned.1.call-start = ((), (), s32[]{:S(2)}) async-start(), calls=%async_computation.2 | async-start | bytes 884736 | tf_op jit(solution)/shard_map/reduce_scatter | solution.py:26
  13.0 2.7 %copy-start.1 = (f32[3072,512]{1,0:T(8,128)}, f32[3072,512]{1,0:T(8,128)S(1)}, u32[]{:S(2)}) copy-start(f32[3072,512]{1,0:T(8,128)S(1)} %convert_add_fusion) | copy-start | bytes 18874372
  22.8 74.6 %all-reduce.2.cloned.1.call-start = ((), (), s32[]{:S(2)}) async-start(), calls=%async_computation.3 | async-start | bytes 196608 | tf_op jit(solution)/shard_map/psum | solution.py:29
  60.7 131.1 %reduce-scatter.5.cloned.1.call-start = ((), (), s32[]{:S(2)}) async-start(), calls=%async_computation.4 | async-start | bytes 294912 | tf_op jit(solution)/shard_map/reduce_scatter | solution.py:33
  145.5 0.9 copy-start.2
Sparse Core Ops, SparseCore 0:
  22.9 37.6 reduce-scatter.2
  63.0 34.4 all-reduce.1
  159.2 32.5 reduce-scatter.4
where the time goes:
time: 239 us
  waiting for transfers between devices  107 us (45%)
  blocking collectives  62.3 us (26%)
  matrix products  34.7 us (15%)
  between operations  13.8 us (6%)
  other arithmetic  12.1 us (5%)
  local copies, waits for them, and re-layouts  8.29 us (3%)
    reduce_scatter x1, waiting for transfers between devices, body(): lax.psum_scatter(jnp.dot(merged, previous_q, precision=HI), 'dev', scatte...  37.8 us
    psum x1, waiting for transfers between devices, body(): p_share = lax.psum(p_share, 'cuts')  36.7 us
    reduce_scatter x1, waiting for transfers between devices, body(): lax.psum_scatter(contract_rows(merged, p_hat), 'dev', scatter_dimension=0...  32.7 us
    psum x1, blocking collectives, body(): gram = lax.psum(contract_rows(p_share, p_share), 'dev')  22.4 us
    psum x1, blocking collectives, body(): q_share = lax.psum(q_share, 'cuts')  19.6 us
    dot_general x2, matrix products, contract_rows(): lax.dot_general(left, right, (((0,), (0,)), ((), ())), precision=HI, pref...  13.9 us
    all_gather x1, blocking collectives, body(): p_hat = lax.all_gather(hat_share, 'dev', axis=0, tiled=True)  11.1 us
    all_gather x1, blocking collectives, body(): q_sum = lax.all_gather(q_share, 'dev', axis=0, tiled=True)  9.24 us
  transfers between devices with their start and end apart: 3, of which 3 were waited for; matrix products, arithmetic and copies ran while one was open for 0% of the time, Pallas kernels for 0%

commit v1 on v0

--- a/solution.py
+++ b/solution.py
@@ -26,7 +26,9 @@
     p_share = lax.psum_scatter(
         jnp.dot(merged, previous_q, precision=HI), "dev", scatter_dimension=0, tiled=True
     )
-    p_share = lax.psum(p_share, "cuts")
+    p_share = p_share
+    for hop in (1, 2):
+        p_share = p_share + lax.ppermute(p_share, "cuts", [(dev, dev ^ hop) for dev in range(4)])
     gram = lax.psum(contract_rows(p_share, p_share), "dev")
     hat_share = solve_factor(gram, p_share)
     p_hat = lax.all_gather(hat_share, "dev", axis=0, tiled=True)

time: 239 us -> 214 us (0.90)
  waiting for transfers between devices: 107 us -> 79.1 us
  starting transfers between devices: 0.12 us -> 4.04 us
    psum x1 -> x0, waiting for transfers between devices: 36.7 us -> none  [body(): p_share = lax.psum(p_share, 'cuts')]
    ppermute x0 -> x2, waiting for transfers between devices: none -> 7.5 us  [body(): lax.ppermute(p_share, 'cuts', [(dev, dev ^ hop) for dev in range(4)])]
    ppermute x0 -> x2, starting transfers between devices: none -> 3.96 us  [body(): lax.ppermute(p_share, 'cuts', [(dev, dev ^ hop) for dev in range(4)])]
  transfers between devices with their start and end apart: 3 -> 4, of which waited for: 3 -> 4; matrix products, arithmetic and copies ran while one was open for 0% -> 0% of each run, Pallas kernels for 0% -> 0%
where the time goes in v1:
time: 214 us
  waiting for transfers between devices  79.1 us (37%)
  blocking collectives  62.3 us (29%)
  matrix products  32.9 us (15%)
  between operations  14.1 us (7%)
  other arithmetic  13 us (6%)
  local copies, waits for them, and re-layouts  8.29 us (4%)
  starting transfers between devices  4.04 us (2%)
    reduce_scatter x1, waiting for transfers between devices, body(): lax.psum_scatter(jnp.dot(merged, previous_q, precision=HI), 'dev', scatte...  37.8 us
    reduce_scatter x1, waiting for transfers between devices, body(): lax.psum_scatter(contract_rows(merged, p_hat), 'dev', scatter_dimension=0...  33.8 us
    psum x1, blocking collectives, body(): gram = lax.psum(contract_rows(p_share, p_share), 'dev')  22.4 us
    psum x1, blocking collectives, body(): q_share = lax.psum(q_share, 'cuts')  19.6 us
    dot_general x2, matrix products, contract_rows(): lax.dot_general(left, right, (((0,), (0,)), ((), ())), precision=HI, pref...  13 us
    all_gather x1, blocking collectives, body(): p_hat = lax.all_gather(hat_share, 'dev', axis=0, tiled=True)  11.1 us
    all_gather x1, blocking collectives, body(): q_sum = lax.all_gather(q_share, 'dev', axis=0, tiled=True)  9.25 us
    dot_general x1, matrix products, body(): approx = jnp.dot(p_hat, q_mean.T, precision=HI)  8.56 us
  transfers between devices with their start and end apart: 4, of which 4 were waited for; matrix products, arithmetic and copies ran while one was open for 0% of the time, Pallas kernels for 0%

profile of v1, /device:TPU:0, one launch (start us, length us, event | category | flops | bytes accessed | tf_op | source)
XLA Modules:
  0.0 213.8 jit_solution(2686181883835082658)
XLA Ops:
  7.2 0.0 copy-start
  7.2 0.0 copy-start.3
  7.2 0.0 reduce-scatter.3.cloned.1.call-start
  7.2 1.8 copy-done
  9.1 4.0 %convert_add_fusion = f32[3072,512]{1,0:T(8,128)S(1)} fusion(bf16[512,3072]{1,0:T(8,128)(2,1)S(1)} %copy-done, bf16[512,512]{1,0:T(8,128)(2,1)} %param.5, bf16[1,3072,512]{2,1,0:T(8,128)(2,1)} %param.6), kind=kOutput, calls=%fused_computation | convolution fusion | flops 1613758464 | bytes 13107200 | tf_op jit(solution)/shard_map/dot_general | solution.py:21
  13.0 0.0 copy-start.1
  13.1 2.7 %copy-done.1 = f32[3072,512]{1,0:T(8,128)} copy-done((f32[3072,512]{1,0:T(8,128)}, f32[3072,512]{1,0:T(8,128)S(1)}, u32[]{:S(2)}) %copy-start.1) | copy-done | bytes 6291480
  15.7 0.0 copy-done.3
  15.7 7.1 %fusion.5 = f32[3072,64]{0,1:T(8,128)} fusion(f32[3072,512]{1,0:T(8,128)S(1)} %convert_add_fusion, f32[512,64]{0,1:T(8,128)S(1)} %copy-done.3), kind=kOutput, calls=%fused_computation.14 | convolution fusion | flops 1207959552 | bytes 7208960 | tf_op jit(solution)/shard_map/dot_general | solution.py:27
  22.8 0.0 reduce-scatter.3.cloned.1.call-update
  22.8 0.0 reduce-scatter.5.cloned.1.call-start
  22.9 37.8 %reduce-scatter.3.cloned.1.call-done = f32[384,64]{0,1:T(8,128)} async-done(((f32[3072,64]{0,1:T(8,128)}), f32[384,64]{0,1:T(8,128)}) %reduce-scatter.3.cloned.1.call-update) | async-done | bytes 98320 | tf_op jit(solution)/shard_map/reduce_scatter | solution.py:26
  60.6 1.5 collective-permute-start
  62.1 3.3 %collective-permute-done = f32[384,64]{0,1:T(8,128)S(1)} collective-permute-done((f32[384,64]{0,1:T(8,128)}, f32[384,64]{0,1:T(8,128)S(1)}, u32[]{:S(2)}, u32[]{:S(2)}) %collective-permute-start) | collective-permute-done | bytes 98336 | tf_op jit(solution)/shard_map/ppermute | solution.py:31
  65.5 0.9 add.29
  66.4 2.5 %collective-permute-start.1 = (f32[384,64]{0,1:T(8,128)S(1)}, f32[384,64]{0,1:T(8,128)S(1)}, u32[]{:S(2)}, u32[]{:S(2)}) collective-permute-start(f32[384,64]{0,1:T(8,128)S(1)} %add.29), channel_id=1, source_target_pairs={{0,16},{8,24},{16,0},{24,8},{1,17},{9,25},{17,1},{25,9},{2,18},{10... | collective-permute-start | bytes 294920 | tf_op jit(solution)/shard_map/ppermute | solution.py:31
  68.9 4.2 %collective-permute-done.1 = f32[384,64]{0,1:T(8,128)S(1)} collective-permute-done((f32[384,64]{0,1:T(8,128)S(1)}, f32[384,64]{0,1:T(8,128)S(1)}, u32[]{:S(2)}, u32[]{:S(2)}) %collective-permute-start.1) | collective-permute-done | bytes 98336 | tf_op jit(solution)/shard_map/ppermute | solution.py:31
  73.0 0.3 fusion.6
  73.3 22.4 %psum.14 = f32[64,64]{0,1:T(8,128)S(1)} all-reduce(f32[64,64]{0,1:T(8,128)S(1)} %fusion.6), channel_id=1, replica_groups=mesh['cuts'=4,'dev'=8] {'dev'}, use_global_device_ids=true, to_apply=%region_1.0 | all-reduce | flops 4096 | bytes 32768 | tf_op jit(solution)/shard_map/psum | solution.py:32
  95.6 0.1 copy.8
  95.7 5.8 %cholesky.16 = f32[64,64]{1,0:T(8,128)S(1)} custom-call(f32[64,64]{1,0:T(8,128)S(1)} %fusion.4), custom_call_target="Cholesky" | custom-call | tf_op jit(solution)/shard_map/jit(cholesky)/cholesky | solution.py:10
  101.6 0.6 compare_reduce_fusion
  102.3 0.7 fusion.1
  102.9 4.9 %custom-call.6 = f32[1,64,64]{1,2,0:T(8,128)S(1)} custom-call(f32[1,64,64]{2,1,0:T(8,128)S(1)} %fusion.1), custom_call_target="InvertDiagBlocksLowerTriangular" | custom-call | tf_op jit(solution)/shard_map/triangular_solve | solution.py:11
  107.8 0.3 fusion.2
  108.1 11.1 %all_gather.6 = f32[3072,64]{0,1:T(8,128)S(1)} all-gather(f32[384,64]{0,1:T(8,128)S(1)} %fusion.2), channel_id=1, replica_groups=mesh['cuts'=4,'dev'=8] {'dev'}, dimensions={0}, use_global_device_ids=true | all-gather | bytes 884736 | tf_op jit(solution)/shard_map/all_gather | solution.py:34
  119.2 0.0 copy-start.2
  119.2 0.9 copy-done.2
  120.1 12.7 %fusion.7 = f32[512,64]{1,0:T(8,128)} fusion(f32[3072,512]{1,0:T(8,128)} %copy-done.1, f32[3072,64]{0,1:T(8,128)S(1)} %all_gather.6), kind=kOutput, calls=%fused_computation.16 | convolution fusion | flops 1207959552 | bytes 7208960 | tf_op jit(solution)/shard_map/dot_general | solution.py:15
  132.8 0.0 reduce-scatter.5.cloned.1.call-update
  132.8 33.8 %reduce-scatter.5.cloned.1.call-done = f32[64,64]{1,0:T(8,128)} async-done(((f32[512,64]{1,0:T(8,128)}), f32[64,64]{1,0:T(8,128)}) %reduce-scatter.5.cloned.1.call-update) | async-done | bytes 16400 | tf_op jit(solution)/shard_map/reduce_scatter | solution.py:35
  166.6 19.6 %psum.15 = f32[64,64]{1,0:T(8,128)S(1)} all-reduce(f32[64,64]{1,0:T(8,128)} %reduce-scatter.5.cloned.1.call-done), channel_id=1, replica_groups=mesh['cuts'=4,'dev'=8] {'cuts'}, use_global_device_ids=true, to_apply=%region_5.6 | all-reduce | flops 4096 | bytes 32768 | tf_op jit(solution)/shard_map/psum | solution.py:36
  186.2 9.2 %all_gather.7 = f32[512,64]{1,0:T(8,128)S(1)} all-gather(f32[64,64]{1,0:T(8,128)S(1)} %psum.15), channel_id=1, replica_groups=mesh['cuts'=4,'dev'=8] {'dev'}, dimensions={0}, use_global_device_ids=true | all-gather | bytes 147456 | tf_op jit(solution)/shard_map/all_gather | solution.py:37
  195.5 8.6 %fusion = bf16[1,3072,512]{2,1,0:T(8,128)(2,1)} fusion(f32[3072,512]{1,0:T(8,128)} %copy-done.1, f32[3072,64]{0,1:T(8,128)} %copy-done.2, f32[512,64]{1,0:T(8,128)S(1)} %all_gather.7), kind=kOutput, calls=%fused_computation.2 | convolution fusion | flops 1211138048 | bytes 10354688 | tf_op jit(solution)/shard_map/dot_general | solution.py:39
  204.1 0.8 copy.9
  204.8 2.1 copy.12
  (4 shorter events, 0.1 us)
Async XLA Ops:
  7.2 1.9 copy-start
  7.2 8.5 %copy-start.3 = (f32[512,64]{0,1:T(8,128)S(1)}, f32[512,64]{0,1:T(8,128)}, u32[]{:S(2)}) copy-start(f32[512,64]{0,1:T(8,128)} %param.7) | copy-start | bytes 393220
  7.2 53.5 %reduce-scatter.3.cloned.1.call-start = ((), (), s32[]{:S(2)}) async-start(), calls=%async_computation.2 | async-start | bytes 884736 | tf_op jit(solution)/shard_map/reduce_scatter | solution.py:26
  13.0 2.7 %copy-start.1 = (f32[3072,512]{1,0:T(8,128)}, f32[3072,512]{1,0:T(8,128)S(1)}, u32[]{:S(2)}) copy-start(f32[3072,512]{1,0:T(8,128)S(1)} %convert_add_fusion) | copy-start | bytes 18874372
  22.8 143.8 %reduce-scatter.5.cloned.1.call-start = ((), (), s32[]{:S(2)}) async-start(), calls=%async_computation.3 | async-start | bytes 294912 | tf_op jit(solution)/shard_map/reduce_scatter | solution.py:35
  60.6 4.8 %collective-permute-start = (f32[384,64]{0,1:T(8,128)}, f32[384,64]{0,1:T(8,128)S(1)}, u32[]{:S(2)}, u32[]{:S(2)}) collective-permute-start(f32[384,64]{0,1:T(8,128)} %reduce-scatter.3.cloned.1.call-done), channel_id=1, source_target_pairs={{0,8},{8,0},{16,24},{24,16},{1,9},{9,1},{17,25},{25,17},{2,10},{10... | collective-permute-start | bytes 294920 | tf_op jit(solution)/shard_map/ppermute | solution.py:31
  66.4 6.6 %collective-permute-start.1 = (f32[384,64]{0,1:T(8,128)S(1)}, f32[384,64]{0,1:T(8,128)S(1)}, u32[]{:S(2)}, u32[]{:S(2)}) collective-permute-start(f32[384,64]{0,1:T(8,128)S(1)} %add.29), channel_id=1, source_target_pairs={{0,16},{8,24},{16,0},{24,8},{1,17},{9,25},{17,1},{25,9},{2,18},{10... | collective-permute-start | bytes 294920 | tf_op jit(solution)/shard_map/ppermute | solution.py:31
  119.2 0.9 copy-start.2
Sparse Core Ops, SparseCore 0:
  22.9 37.6 reduce-scatter.2
  132.9 33.6 reduce-scatter.4
